TPU v7x, 32 devices: a whole 2x2x4 slice. The times are simulated.
32 devices in a mesh: gx: 16 (over z, y, core), gy: 2 (over x).
Axes of the slice: x: 2, y: 2, z: 4, core: 2. Of those that a mesh axis runs over, the one named last changes fastest.
Arguments:
- prognostic_values: float32 [3, 6, 2048, 1024], P(None, None, 'gx', 'gy'), may hold values from -6 to 6
- forcing_host_values: bfloat16 [3, 6, 2048, 1024], P(None, None, 'gx', 'gy'), may hold values from -6 to 6
- strength: float32 [3, 6], replicated, may hold values from 50 to 200
- level_height: float32 [3], replicated, may hold values from 0.2 to 3
- pbl_height: float32 [2048, 1024], P('gx', 'gy'), may hold values from 0.2 to 3
Outputs:
- tendency: bfloat16 [3, 6, 2048, 1024], P(None, None, 'gx', 'gy')
- energy: float32 [3, 6], replicated
All inputs are finite; a program needn't handle non-finite values.
Results may differ from a plain program's by a relative error of at most 0.001.
Values sent between devices are 32-bit elements; how exact they have to be, the bound alone decides.
A program may use at most 64 MiB of HBM per device.

v0:
```python
import jax
import jax.numpy as jnp
from jax import lax
from jax.sharding import PartitionSpec as P

KX = 32
KY = 32


ramp_depth = 0.25


def cosine_table(total, modes, start, count):
    index = (start + jnp.arange(count)).astype(jnp.float32)
    waves = jnp.arange(modes).astype(jnp.float32)
    scales = jnp.where(waves == 0.0, jnp.sqrt(1.0 / total), jnp.sqrt(2.0 / total)).astype(
        jnp.float32
    )
    return scales[None, :] * jnp.cos(jnp.pi * (index[:, None] + 0.5) * waves[None, :] / total)


def per_device(prognostic_values, forcing_host_values, strength, level_height, pbl_height):
    rows = prognostic_values.shape[2]
    cols = prognostic_values.shape[3]
    largest_wavenumber = lax.Precision.HIGHEST
    row_table = cosine_table(rows * lax.axis_size("gx"), KX, lax.axis_index("gx") * rows, rows)
    col_table = cosine_table(cols * lax.axis_size("gy"), KY, lax.axis_index("gy") * cols, cols)
    diff = forcing_host_values.astype(jnp.float32) - prognostic_values
    part = jnp.einsum("...ij,jb->...ib", diff, col_table, precision=largest_wavenumber)
    mode_factors = lax.psum(
        jnp.einsum("ia,...ib->...ab", row_table, part, precision=largest_wavenumber), ("gx", "gy")
    )
    restored_fields = jnp.einsum(
        "ia,lvab->lvib", row_table, mode_factors, precision=largest_wavenumber
    )
    recon = jnp.einsum("lvib,jb->lvij", restored_fields, col_table, precision=largest_wavenumber)
    damping_share = 1.0 / (
        1.0 + jnp.exp(-(level_height[:, None, None] - pbl_height[None]) / ramp_depth)
    )
    tendency = (strength[:, :, None, None] * damping_share[:, None] * recon).astype(jnp.bfloat16)
    energy = jnp.sum(mode_factors * mode_factors, axis=(2, 3)) / (KX * KY)
    return (tendency, energy)


def solution(mesh):
    return jax.shard_map(
        per_device,
        mesh=mesh,
        in_specs=(P(None, None, "gx", "gy"), P(None, None, "gx", "gy"), P(), P(), P("gx", "gy")),
        out_specs=(P(None, None, "gx", "gy"), P()),
        check_vma=False,
    )
```

profile of v0, /device:TPU:0, one launch (start us, length us, event | category | flops | bytes accessed | tf_op | source)
XLA Modules:
  0.0 161.5 jit_solution(8054716955889368383)
XLA Ops:
  7.2 0.0 copy-start
  7.2 0.0 copy-start.1
  7.2 0.0 all-reduce.2.cloned.1.call-start
  7.3 0.0 copy-start.2
  7.3 7.3 %fusion = f32[3,6,128,32]{2,3,1,0:T(8,128)S(1)} fusion(f32[3,6,128,512]{3,2,1,0:T(8,128)} %param.5, bf16[3,6,128,512]{3,2,1,0:T(8,128)(2,1)} %param.6, f32[32]{0:T(128)S(1)} %iota_convert_fusion, f32[512]{0:T(512)S(1)} %add_multiply_fusion, f32[32]{0:T(128)S(1)} %compare_select_fusion.1), kind=kOutput, calls=%fused_computation.1 | convolution fusion | flops 455393280 | bytes 7375104 | tf_op jit(solution)/shard_map/...ij,jb->...ib/dot_general | solution.py:29
  14.6 1.2 convolution_bitcast_fusion.1
  15.8 0.0 all-reduce.2.cloned.1.call-update
  15.8 0.0 copy-done
  15.9 0.0 copy-done.1
  15.9 0.3 add_divide_fusion
  16.2 129.6 %all-reduce.2.cloned.1.call-done = f32[3,6,32,32]{2,3,1,0:T(8,128)} async-done(((f32[3,6,32,32]{2,3,1,0:T(8,128)}), f32[3,6,32,32]{2,3,1,0:T(8,128)}) %all-reduce.2.cloned.1.call-update) | async-done | bytes 73744 | tf_op jit(solution)/shard_map/psum | solution.py:30
  145.7 1.1 multiply_reduce_fusion
  146.8 0.6 broadcast_multiply_fusion
  147.4 1.5 convolution_bitcast_fusion
  148.9 0.0 copy-done.2
  148.9 5.8 %multiply_convert_fusion = bf16[3,6,128,512]{3,2,1,0:T(8,128)(2,1)} fusion(f32[3,128,512]{2,1,0:T(8,128)S(1)} %add_divide_fusion, f32[3,6]{1,0:T(4,128)S(1)} %copy-done.2, f32[3,6,128,32]{2,3,1,0:T(8,128)S(1)} %convolution_bitcast_fusion, f32[32]{0:T(128)S(1)} %iota_convert_fusion, f32[512]{0:T(512)S(1)} %add_multiply_fusion, f32[32]{0:T(128)S(1)} %compare_select_fusion.1), kind=kOutput, calls=%fused_computation | convolution fusion | flops 456572928 | bytes 3443016 | tf_op jit(solution)/shard_map/lvib,jb->lvij/dot_general | solution.py:36
  (5 shorter events, 0.0 us)
Async XLA Ops:
  7.2 8.7 %copy-start = (f32[128,512]{1,0:T(8,128)S(1)}, f32[128,512]{1,0:T(8,128)}, u32[]{:S(2)}) copy-start(f32[128,512]{1,0:T(8,128)} %param.9) | copy-start | bytes 786436
  7.2 8.7 %copy-start.1 = (f32[3]{0:T(128)S(1)}, f32[3]{0:T(128)}, u32[]{:S(2)}) copy-start(f32[3]{0:T(128)} %param.8) | copy-start | bytes 40
  7.2 138.5 %all-reduce.2.cloned.1.call-start = ((), (), s32[]{:S(2)}) async-start(), calls=%async_computation | async-start | bytes 589824 | tf_op jit(solution)/shard_map/psum | solution.py:30
  7.3 141.6 %copy-start.2 = (f32[3,6]{1,0:T(4,128)S(1)}, f32[3,6]{1,0:T(4,128)}, u32[]{:S(2)}) copy-start(f32[3,6]{1,0:T(4,128)} %param.7) | copy-start | bytes 220
Sparse Core Ops, SparseCore 0:
  16.0 129.6 all-reduce.1
where the time goes:
time: 162 us; the launch traced here: 161 us
  waiting for transfers between devices  130 us (80%)
  matrix products  15.7 us (10%)
  between operations  14.1 us (9%)
  other arithmetic  2 us (1%)
    psum x1, waiting for transfers between devices, per_device(): lax.psum(jnp.einsum('ia,...ib->...ab', row_table, part, precision=largest...  130 us
    dot_general x1, matrix products, per_device(): jnp.einsum('...ij,jb->...ib', diff, col_table, precision=largest_wavenumber)  7.27 us
    dot_general x1, matrix products, per_device(): jnp.einsum('lvib,jb->lvij', restored_fields, col_table, precision=largest...  5.76 us
  transfers between devices with their start and end apart: 1, of which 1 were waited for; matrix products, arithmetic and copies ran while one was open for 0% of the time, Pallas kernels for 0%

commit v1 on v0

v1 whole, which is shorter than its diff:
```python
import functools
import math

import jax
import jax.numpy as jnp
from jax import lax
from jax.experimental import pallas as pl
from jax.experimental.pallas import tpu as pltpu
from jax.sharding import PartitionSpec as P

KX = 32
KY = 32
RAMP_DEPTH = 0.25
LANES = 128
SUB = 8
MESH = pl.DeviceIdType.MESH

F32 = jnp.float32
BF16 = jnp.bfloat16

SINE = [(-1.0) ** k * (math.pi / 2) ** (2 * k + 1) / math.factorial(2 * k + 1) for k in range(7)]


def basis(total, place, wave):
    turns = (2.0 * place + 1.0) * wave
    rest = turns - (4.0 * total) * jnp.floor(turns * (1.0 / (4.0 * total)))
    t = (jnp.abs(rest - 2.0 * total) - total) * (1.0 / total)
    t2 = t * t
    poly = jnp.full(t.shape, SINE[-1], F32)
    for c in SINE[-2::-1]:
        poly = poly * t2 + c
    scale = jnp.where(wave == 0.0, math.sqrt(1.0 / total), math.sqrt(2.0 / total))
    return scale * (poly * t)


def iota(shape, dim):
    return lax.broadcasted_iota(jnp.int32, shape, dim)


def split(x):
    hi = x.astype(BF16)
    return hi, (x - hi.astype(F32)).astype(BF16)


def group_masks(rows):
    lane = iota((rows, LANES), 1) // KY
    return [lane == g for g in range(LANES // KY)]


def analysis_kernel(
    dims, prog_hbm, forc_hbm, coef_ref,
    prog, forc, part, mine, got_in, total, got_out, full,
    prog_sem, forc_sem, in_send, in_recv, out_send, out_recv, all_send, all_recv,
):
    gx, gy, n_mid, chunk = dims
    fields, rows, cols = prog.shape
    n_chunks = fields // chunk
    groups = KX // SUB
    n_in, n_out = n_mid * gy, gx // n_mid
    ix, iy = lax.axis_index("gx"), lax.axis_index("gy")
    outer, mid = ix // n_mid, lax.rem(ix, n_mid)
    me = mid * gy + iy

    def fetch(c):
        span = pl.ds(c * chunk, chunk)
        return (
            pltpu.make_async_copy(prog_hbm.at[span], prog.at[span], prog_sem.at[c]),
            pltpu.make_async_copy(forc_hbm.at[span], forc.at[span], forc_sem.at[c]),
        )

    for c in range(n_chunks):
        for copy in fetch(c):
            copy.start()

    def inner_peer(d):
        other = lax.rem(me + d, n_in)
        return other, (outer * n_mid + other // gy, lax.rem(other, gy))

    def outer_peer(d):
        return (lax.rem(outer + d, n_out) * n_mid + mid, iy)

    barrier = pltpu.get_barrier_semaphore()
    for d in range(1, n_in):
        pl.semaphore_signal(barrier, inc=1, device_id=inner_peer(d)[1], device_id_type=MESH)
    for d in range(1, n_out):
        pl.semaphore_signal(barrier, inc=1, device_id=outer_peer(d), device_id_type=MESH)

    row = basis(
        rows * gx,
        (ix * rows + iota((KX, rows), 1)).astype(F32),
        iota((KX, rows), 0).astype(F32),
    )
    row_hi, row_lo = split(row)
    row_lhs = jnp.concatenate([row_hi, row_lo], axis=0)
    row_lhs = jnp.concatenate([row_lhs, row_lhs], axis=1)
    col = basis(
        cols * gy,
        (iy * cols + iota((cols, LANES), 0)).astype(F32),
        lax.rem(iota((cols, LANES), 1), KY).astype(F32),
    )
    col_rhs = jnp.concatenate(split(col), axis=1)

    def one_chunk(c, carry):
        for copy in fetch(c):
            copy.wait()
        for k in range(chunk):
            f = c * chunk + k
            diff = forc[f].astype(F32) - prog[f]
            rhs = jnp.concatenate(split(diff), axis=0)
            both = jnp.dot(row_lhs, rhs, preferred_element_type=F32)
            both = both[:KX] + both[KX:]
            for g in range(groups):
                part[g, f] = both[g * SUB:(g + 1) * SUB]
        return carry

    lax.fori_loop(0, n_chunks, one_chunk, 0)

    hi, lo = split(part[...].reshape(groups * fields * SUB, cols))
    both = jnp.dot(hi, col_rhs, preferred_element_type=F32) + jnp.dot(
        lo, col_rhs, preferred_element_type=F32
    )
    both = both[:, :LANES] + both[:, LANES:]
    size = fields * SUB
    coef = both[:size]
    for g, mask in list(enumerate(group_masks(size)))[1:]:
        coef = jnp.where(mask, both[g * size:(g + 1) * size], coef)
    slots = mine.shape[0]
    for f in range(slots * n_in):
        if f < fields:
            mine[f // n_in, f % n_in] = coef[f * SUB:(f + 1) * SUB]
        else:
            mine[f // n_in, f % n_in] = jnp.zeros((SUB, LANES), F32)

    pl.semaphore_wait(barrier, n_in - 1 + n_out - 1)

    copies = []
    for d in range(1, n_in):
        other, device = inner_peer(d)
        copies.append(pltpu.make_async_remote_copy(
            src_ref=mine.at[:, other], dst_ref=got_in.at[d - 1],
            send_sem=in_send.at[d - 1], recv_sem=in_recv.at[d - 1],
            device_id=device, device_id_type=MESH,
        ))
        copies[-1].start()
    acc = mine[:, me]
    for d, copy in enumerate(copies):
        copy.wait_recv()
        acc = acc + got_in[d]
    total[...] = acc
    outs = []
    for d in range(1, n_out):
        outs.append(pltpu.make_async_remote_copy(
            src_ref=total, dst_ref=got_out.at[d - 1],
            send_sem=out_send.at[d - 1], recv_sem=out_recv.at[d - 1],
            device_id=outer_peer(d), device_id_type=MESH,
        ))
        outs[-1].start()
    for d, copy in enumerate(outs):
        copy.wait_recv()
        acc = acc + got_out[d]
    full[:, me] = acc
    alls = []
    for d in range(1, n_in):
        alls.append(pltpu.make_async_remote_copy(
            src_ref=full.at[:, me], dst_ref=full.at[:, me],
            send_sem=all_send.at[d - 1], recv_sem=all_recv.at[d - 1],
            device_id=inner_peer(d)[1], device_id_type=MESH,
        ))
        alls[-1].start()
    for copy in alls:
        copy.wait_recv()
    for f in range(fields):
        coef_ref[f * SUB:(f + 1) * SUB] = full[f // n_in, f % n_in]
    for copy in copies + outs + alls:
        copy.wait_send()


def synthesis_kernel(
    dims, strength_ref, level_ref, coef_ref, pbl_ref, tend_hbm, energy_ref,
    wave, weight, tend, tend_sem,
):
    gx, gy = dims
    levels, variables, rows, cols = tend.shape
    fields = levels * variables
    groups = KX // SUB
    ix, iy = lax.axis_index("gx"), lax.axis_index("gy")

    coef = coef_ref[...]
    size = fields * SUB
    stack = jnp.concatenate([jnp.where(m, coef, 0.0) for m in group_masks(size)], axis=0)
    hi, lo = split(stack)
    lhs = jnp.concatenate([hi, lo, hi], axis=1)
    col_hi, col_lo = split(basis(
        cols * gy,
        (iy * cols + iota((LANES, cols), 1)).astype(F32),
        lax.rem(iota((LANES, cols), 0), KY).astype(F32),
    ))
    rhs = jnp.concatenate([col_hi, col_hi, col_lo], axis=0)
    wave[...] = jnp.dot(lhs, rhs, preferred_element_type=F32).reshape(
        groups, fields, SUB, cols
    )

    row_hi, row_lo = split(basis(
        rows * gx,
        (ix * rows + iota((rows, 4 * KX), 0)).astype(F32),
        lax.rem(iota((rows, 4 * KX), 1), KX).astype(F32),
    ))
    row_lhs = jnp.where(iota((rows, 4 * KX), 1) < 2 * KX, row_hi.astype(F32), row_lo.astype(F32)).astype(BF16)

    power = coef * coef
    at_row = iota((levels, variables), 0)
    at_col = iota((levels, variables), 1)
    energy = jnp.zeros((levels, variables), F32)
    for l in range(levels):
        for v in range(variables):
            f = l * variables + v
            one = jnp.sum(power[f * SUB:(f + 1) * SUB], axis=(0, 1), keepdims=True)
            energy = jnp.where((at_row == l) & (at_col == v), one, energy)
    energy_ref[...] = energy * (1.0 / (KX * KY))

    def put(l, v):
        return pltpu.make_async_copy(tend.at[l, v], tend_hbm.at[l, v], tend_sem.at[l, v])

    def one_level(l, carry):
        weight[...] = 1.0 / (1.0 + jnp.exp(-(level_ref[l] - pbl_ref[...]) / RAMP_DEPTH))
        for v in range(variables):
            f = l * variables + v
            whole = jnp.concatenate([wave[g, f] for g in range(groups)], axis=0)
            hi, lo = split(whole)
            rhs = jnp.concatenate([hi, lo, hi, lo], axis=0)
            recon = jnp.dot(row_lhs, rhs, preferred_element_type=F32)
            tend[l, v] = (strength_ref[l, v] * weight[...] * recon).astype(BF16)
            if v:
                put(l, v - 1).start()
        put(l, variables - 1).start()
        return carry

    lax.fori_loop(0, levels, one_level, 0)
    for l in range(levels):
        for v in range(variables):
            put(l, v).wait()


def per_device(gx, gy, prognostic_values, forcing_host_values, strength, level_height, pbl_height):
    levels, variables, rows, cols = prognostic_values.shape
    fields = levels * variables
    groups = KX // SUB
    n_mid = math.gcd(gx, 4)
    n_in, n_out = n_mid * gy, gx // n_mid
    slots = -(-fields // n_in)
    chunk = 3 if fields % 3 == 0 else 1
    n_chunks = fields // chunk
    anywhere = pl.BlockSpec(memory_space=pl.ANY)
    vmem = pl.BlockSpec(memory_space=pltpu.VMEM)
    smem = pl.BlockSpec(memory_space=pltpu.SMEM)
    dma = pltpu.SemaphoreType.DMA
    coef = pl.pallas_call(
        functools.partial(analysis_kernel, (gx, gy, n_mid, chunk)),
        out_shape=jax.ShapeDtypeStruct((fields * SUB, LANES), F32),
        in_specs=[anywhere, anywhere],
        out_specs=vmem,
        scratch_shapes=[
            pltpu.VMEM((fields, rows, cols), F32),
            pltpu.VMEM((fields, rows, cols), BF16),
            pltpu.VMEM((groups, fields, SUB, cols), F32),
            pltpu.VMEM((slots, n_in, SUB, LANES), F32),
            pltpu.VMEM((max(n_in - 1, 1), slots, SUB, LANES), F32),
            pltpu.VMEM((slots, SUB, LANES), F32),
            pltpu.VMEM((max(n_out - 1, 1), slots, SUB, LANES), F32),
            pltpu.VMEM((slots, n_in, SUB, LANES), F32),
            dma((n_chunks,)),
            dma((n_chunks,)),
            dma((max(n_in - 1, 1),)),
            dma((max(n_in - 1, 1),)),
            dma((max(n_out - 1, 1),)),
            dma((max(n_out - 1, 1),)),
            dma((max(n_in - 1, 1),)),
            dma((max(n_in - 1, 1),)),
        ],
        compiler_params=pltpu.CompilerParams(collective_id=0, has_side_effects=True),
        name="analysis",
    )(
        prognostic_values.reshape(fields, rows, cols),
        forcing_host_values.reshape(fields, rows, cols),
    )
    tendency, energy = pl.pallas_call(
        functools.partial(synthesis_kernel, (gx, gy)),
        out_shape=(
            jax.ShapeDtypeStruct((levels, variables, rows, cols), BF16),
            jax.ShapeDtypeStruct((levels, variables), F32),
        ),
        in_specs=[smem, smem, vmem, vmem],
        out_specs=(anywhere, vmem),
        scratch_shapes=[
            pltpu.VMEM((groups, fields, SUB, cols), F32),
            pltpu.VMEM((rows, cols), F32),
            pltpu.VMEM((levels, variables, rows, cols), BF16),
            dma((levels, variables)),
        ],
        name="synthesis",
    )(strength, level_height, coef, pbl_height)
    return tendency, energy


def solution(mesh):
    return jax.shard_map(
        functools.partial(per_device, mesh.shape["gx"], mesh.shape["gy"]),
        mesh=mesh,
        in_specs=(P(None, None, "gx", "gy"), P(None, None, "gx", "gy"), P(), P(), P("gx", "gy")),
        out_specs=(P(None, None, "gx", "gy"), P()),
        check_vma=False,
    )
```

time: 162 us -> 23.8 us (0.15)
  waiting for transfers between devices: 130 us -> 0 us
  Pallas kernels: 0 us -> 23 us
  matrix products: 15.7 us -> 0 us
  between operations: 14.1 us -> 0.64 us
  other arithmetic: 2 us -> 0 us
    psum x1 -> x0, waiting for transfers between devices: 130 us -> none  [per_device(): lax.psum(jnp.einsum('ia,...ib->...ab', row_table, part, precision=largest...]
    pallas_call x0 -> x2, Pallas kernels: none -> 23 us  [the longest x1 18.7 us: per_device(): pl.pallas_call(functools.partial(analysis_kernel, (gx, gy, n_mid, chunk))...]
    dot_general x4 -> x0, matrix products: 15.7 us -> none  [the longest x1 7.27 us: per_device(): jnp.einsum('...ij,jb->...ib', diff, col_table, precision=largest_wavenumber)]
  transfers between devices with their start and end apart: 1 -> 0, of which waited for: 1 -> 0; matrix products, arithmetic and copies ran while one was open for 0% -> 0% of each run, Pallas kernels for 0% -> 0%
where the time goes in v1:
time: 23.8 us; the launch traced here: 23.7 us
  Pallas kernels  23 us (97%)
  between operations  0.64 us (3%)
    pallas_call x1, Pallas kernels, per_device(): pl.pallas_call(functools.partial(analysis_kernel, (gx, gy, n_mid, chunk))...  18.7 us
    pallas_call x1, Pallas kernels, per_device(): pl.pallas_call(functools.partial(synthesis_kernel, (gx, gy)), out_shape=(...  4.34 us

profile of v1, /device:TPU:0, one launch (start us, length us, event | category | flops | bytes accessed | tf_op | source)
XLA Modules:
  0.0 23.7 jit_solution(6395655997226533849)
XLA Ops:
  0.6 18.7 %analysis.1.coef_ref = f32[144,128]{1,0:T(8,128)} custom-call(f32[18,128,512]{2,1,0:T(8,128)} %bitcast.2, bf16[18,128,512]{2,1,0:T(8,128)(2,1)} %bitcast.3), custom_call_target="tpu_custom_call" | custom-call | tf_op jit(solution)/shard_map/analysis/pallas_call | solution.py:257
  19.3 4.3 %synthesis.1 = (bf16[3,6,128,512]{3,2,1,0:T(8,128)(2,1)}, f32[3,6]{1,0:T(4,128)}) custom-call(f32[3,6]{1,0:T(4,128)} %strength_ref.1, f32[3]{0:T(128)} %level_ref.1, f32[144,128]{1,0:T(8,128)} %analysis.1.coef_ref, f32[128,512]{1,0:T(8,128)} %pbl_ref.1), custom_call_target="tpu_custom_call" | custom-call | tf_op jit(solution)/shard_map/synthesis/pallas_call | solution.py:286

commit v2 on v1

--- a/solution.py
+++ b/solution.py
@@ -48,9 +48,10 @@
 
 
 def analysis_kernel(
-    dims, prog_hbm, forc_hbm, coef_ref,
-    prog, forc, part, mine, got_in, total, got_out, full,
-    prog_sem, forc_sem, in_send, in_recv, out_send, out_recv, all_send, all_recv,
+    dims, prog_hbm, forc_hbm, strength_hbm, level_hbm, pbl_hbm,
+    coef_ref, scale_ref, weight_ref, row_ref, col_ref,
+    strength, level, pbl, prog, forc, part, mine, got_in, total, got_out, full,
+    prog_sem, forc_sem, aux_sem, in_send, in_recv, out_send, out_recv, all_send, all_recv,
 ):
     gx, gy, n_mid, chunk = dims
     fields, rows, cols = prog.shape
@@ -71,6 +72,13 @@
     for c in range(n_chunks):
         for copy in fetch(c):
             copy.start()
+    aux = [
+        pltpu.make_async_copy(pbl_hbm, pbl, aux_sem.at[0]),
+        pltpu.make_async_copy(strength_hbm, strength, aux_sem.at[1]),
+        pltpu.make_async_copy(level_hbm, level, aux_sem.at[2]),
+    ]
+    for copy in aux:
+        copy.start()
 
     def inner_peer(d):
         other = lax.rem(me + d, n_in)
@@ -142,6 +150,29 @@
             device_id=device, device_id_type=MESH,
         ))
         copies[-1].start()
+    for copy in aux:
+        copy.wait()
+    levels, variables = strength.shape
+    for l in range(levels):
+        weight_ref[l] = 1.0 / (1.0 + jnp.exp(-(level[l] - pbl[...]) / RAMP_DEPTH))
+        for v in range(variables):
+            f = l * variables + v
+            scale_ref[f * SUB:(f + 1) * SUB] = jnp.full((SUB, LANES), strength[l, v], F32)
+    col_hi, col_lo = split(basis(
+        cols * gy,
+        (iy * cols + iota((LANES, cols), 1)).astype(F32),
+        lax.rem(iota((LANES, cols), 0), KY).astype(F32),
+    ))
+    col_ref[...] = jnp.concatenate([col_hi, col_hi, col_lo], axis=0)
+    row_hi, row_lo = split(basis(
+        rows * gx,
+        (ix * rows + iota((rows, 4 * KX), 0)).astype(F32),
+        lax.rem(iota((rows, 4 * KX), 1), KX).astype(F32),
+    ))
+    row_ref[...] = jnp.where(
+        iota((rows, 4 * KX), 1) < 2 * KX, row_hi.astype(F32), row_lo.astype(F32)
+    ).astype(BF16)
+
     acc = mine[:, me]
     for d, copy in enumerate(copies):
         copy.wait_recv()
@@ -176,36 +207,39 @@
 
 
 def synthesis_kernel(
-    dims, strength_ref, level_ref, coef_ref, pbl_ref, tend_hbm, energy_ref,
-    wave, weight, tend, tend_sem,
+    coef_ref, scale_ref, weight_ref, row_ref, col_ref, tend_hbm, energy_ref, wave, tend, tend_sem,
 ):
-    gx, gy = dims
     levels, variables, rows, cols = tend.shape
     fields = levels * variables
     groups = KX // SUB
-    ix, iy = lax.axis_index("gx"), lax.axis_index("gy")
 
     coef = coef_ref[...]
     size = fields * SUB
-    stack = jnp.concatenate([jnp.where(m, coef, 0.0) for m in group_masks(size)], axis=0)
+    scaled = coef * scale_ref[...]
+    stack = jnp.concatenate([jnp.where(m, scaled, 0.0) for m in group_masks(size)], axis=0)
     hi, lo = split(stack)
     lhs = jnp.concatenate([hi, lo, hi], axis=1)
-    col_hi, col_lo = split(basis(
-        cols * gy,
-        (iy * cols + iota((LANES, cols), 1)).astype(F32),
-        lax.rem(iota((LANES, cols), 0), KY).astype(F32),
-    ))
-    rhs = jnp.concatenate([col_hi, col_hi, col_lo], axis=0)
-    wave[...] = jnp.dot(lhs, rhs, preferred_element_type=F32).reshape(
+    wave[...] = jnp.dot(lhs, col_ref[...], preferred_element_type=F32).reshape(
         groups, fields, SUB, cols
     )
 
-    row_hi, row_lo = split(basis(
-        rows * gx,
-        (ix * rows + iota((rows, 4 * KX), 0)).astype(F32),
-        lax.rem(iota((rows, 4 * KX), 1), KX).astype(F32),
-    ))
-    row_lhs = jnp.where(iota((rows, 4 * KX), 1) < 2 * KX, row_hi.astype(F32), row_lo.astype(F32)).astype(BF16)
+    def put(l, v):
+        return pltpu.make_async_copy(tend.at[l, v], tend_hbm.at[l, v], tend_sem.at[l, v])
+
+    def one_level(l, carry):
+        for v in range(variables):
+            f = l * variables + v
+            whole = jnp.concatenate([wave[g, f] for g in range(groups)], axis=0)
+            hi, lo = split(whole)
+            rhs = jnp.concatenate([hi, lo, hi, lo], axis=0)
+            recon = jnp.dot(row_ref[...], rhs, preferred_element_type=F32)
+            tend[l, v] = (weight_ref[l] * recon).astype(BF16)
+            if v:
+                put(l, v - 1).start()
+        put(l, variables - 1).start()
+        return carry
+
+    lax.fori_loop(0, levels, one_level, 0)
 
     power = coef * coef
     at_row = iota((levels, variables), 0)
@@ -218,24 +252,6 @@
             energy = jnp.where((at_row == l) & (at_col == v), one, energy)
     energy_ref[...] = energy * (1.0 / (KX * KY))
 
-    def put(l, v):
-        return pltpu.make_async_copy(tend.at[l, v], tend_hbm.at[l, v], tend_sem.at[l, v])
-
-    def one_level(l, carry):
-        weight[...] = 1.0 / (1.0 + jnp.exp(-(level_ref[l] - pbl_ref[...]) / RAMP_DEPTH))
-        for v in range(variables):
-            f = l * variables + v
-            whole = jnp.concatenate([wave[g, f] for g in range(groups)], axis=0)
-            hi, lo = split(whole)
-            rhs = jnp.concatenate([hi, lo, hi, lo], axis=0)
-            recon = jnp.dot(row_lhs, rhs, preferred_element_type=F32)
-            tend[l, v] = (strength_ref[l, v] * weight[...] * recon).astype(BF16)
-            if v:
-                put(l, v - 1).start()
-        put(l, variables - 1).start()
-        return carry
-
-    lax.fori_loop(0, levels, one_level, 0)
     for l in range(levels):
         for v in range(variables):
             put(l, v).wait()
@@ -252,14 +268,22 @@
     n_chunks = fields // chunk
     anywhere = pl.BlockSpec(memory_space=pl.ANY)
     vmem = pl.BlockSpec(memory_space=pltpu.VMEM)
-    smem = pl.BlockSpec(memory_space=pltpu.SMEM)
     dma = pltpu.SemaphoreType.DMA
-    coef = pl.pallas_call(
+    held = pl.pallas_call(
         functools.partial(analysis_kernel, (gx, gy, n_mid, chunk)),
-        out_shape=jax.ShapeDtypeStruct((fields * SUB, LANES), F32),
-        in_specs=[anywhere, anywhere],
-        out_specs=vmem,
+        out_shape=(
+            pltpu.VMEM((fields * SUB, LANES), F32),
+            pltpu.VMEM((fields * SUB, LANES), F32),
+            pltpu.VMEM((levels, rows, cols), F32),
+            pltpu.VMEM((rows, 4 * KX), BF16),
+            pltpu.VMEM((3 * LANES, cols), BF16),
+        ),
+        in_specs=[anywhere] * 5,
+        out_specs=(vmem,) * 5,
         scratch_shapes=[
+            pltpu.SMEM((levels, variables), F32),
+            pltpu.SMEM((levels,), F32),
+            pltpu.VMEM((rows, cols), F32),
             pltpu.VMEM((fields, rows, cols), F32),
             pltpu.VMEM((fields, rows, cols), BF16),
             pltpu.VMEM((groups, fields, SUB, cols), F32),
@@ -270,6 +294,7 @@
             pltpu.VMEM((slots, n_in, SUB, LANES), F32),
             dma((n_chunks,)),
             dma((n_chunks,)),
+            dma((3,)),
             dma((max(n_in - 1, 1),)),
             dma((max(n_in - 1, 1),)),
             dma((max(n_out - 1, 1),)),
@@ -282,23 +307,25 @@
     )(
         prognostic_values.reshape(fields, rows, cols),
         forcing_host_values.reshape(fields, rows, cols),
+        strength,
+        level_height,
+        pbl_height,
     )
     tendency, energy = pl.pallas_call(
-        functools.partial(synthesis_kernel, (gx, gy)),
+        synthesis_kernel,
         out_shape=(
             jax.ShapeDtypeStruct((levels, variables, rows, cols), BF16),
             jax.ShapeDtypeStruct((levels, variables), F32),
         ),
-        in_specs=[smem, smem, vmem, vmem],
+        in_specs=[vmem] * 5,
         out_specs=(anywhere, vmem),
         scratch_shapes=[
             pltpu.VMEM((groups, fields, SUB, cols), F32),
-            pltpu.VMEM((rows, cols), F32),
             pltpu.VMEM((levels, variables, rows, cols), BF16),
             dma((levels, variables)),
         ],
         name="synthesis",
-    )(strength, level_height, coef, pbl_height)
+    )(*[pltpu.with_memory_space_constraint(x, pltpu.VMEM) for x in held])
     return tendency, energy
 
 

time: 23.8 us -> 22 us (0.924)
  Pallas kernels: 23 us -> 21.2 us
    pallas_call x1, Pallas kernels: 4.34 us -> 3.03 us  [per_device(): pl.pallas_call(synthesis_kernel, out_shape=(jax.ShapeDtypeStruct((levels,...]
    pallas_call x1, Pallas kernels: 18.7 us -> 18.1 us  [per_device(): pl.pallas_call(functools.partial(analysis_kernel, (gx, gy, n_mid, chunk))...]
where the time goes in v2:
time: 22 us; the launch traced here: 21.8 us
  Pallas kernels  21.2 us (96%)
  between operations  0.64 us (3%)
    pallas_call x1, Pallas kernels, per_device(): pl.pallas_call(functools.partial(analysis_kernel, (gx, gy, n_mid, chunk))...  18.1 us
    pallas_call x1, Pallas kernels, per_device(): pl.pallas_call(synthesis_kernel, out_shape=(jax.ShapeDtypeStruct((levels,...  3.03 us

profile of v2, /device:TPU:0, one launch (start us, length us, event | category | flops | bytes accessed | tf_op | source)
XLA Modules:
  0.0 21.8 jit_solution(8245589834449547687)
XLA Ops:
  0.6 18.1 %analysis.1 = (f32[144,128]{1,0:T(8,128)S(1)}, f32[144,128]{1,0:T(8,128)S(1)}, f32[3,128,512]{2,1,0:T(8,128)S(1)}, bf16[128,128]{1,0:T(8,128)(2,1)S(1)}, bf16[384,512]{1,0:T(8,128)(2,1)S(1)}) custom-call(f32[18,128,512]{2,1,0:T(8,128)} %bitcast.2, bf16[18,128,512]{2,1,0:T(8,128)(2,1)} %bitcast.3, f32[3,6]{1,0:T(4,128)} %strength_hbm.1, f32[3]{0:T(128)} %level_hbm.1, ...), custom_call_target="tpu_custom_call" | custom-call | tf_op jit(solution)/shard_map/analysis/pallas_call | solution.py:272
  18.8 3.0 %synthesis.1 = (bf16[3,6,128,512]{3,2,1,0:T(8,128)(2,1)}, f32[3,6]{1,0:T(4,128)}) custom-call(f32[144,128]{1,0:T(8,128)S(1)} %get-tuple-element.7.coef_ref, f32[144,128]{1,0:T(8,128)S(1)} %get-tuple-element.8.scale_ref, f32[3,128,512]{2,1,0:T(8,128)S(1)} %get-tuple-element.9.weight_ref, bf16[128,128]{1,0:T(8,128)(2,1)S(1)} %get-tuple-element.10.row_ref, ...), custom_call_target="tpu_custom_call" | custom-call | tf_op jit(solution)/shard_map/synthesis/pallas_call | solution.py:314

commit v3 on v2

v3 whole, which is shorter than its diff:
```python
import functools
import math

import jax
import jax.numpy as jnp
from jax import lax
from jax.experimental import pallas as pl
from jax.experimental.pallas import tpu as pltpu
from jax.sharding import PartitionSpec as P

KX = 32
KY = 32
RAMP_DEPTH = 0.25
LANES = 128
SUB = 8
MESH = pl.DeviceIdType.MESH

F32 = jnp.float32
BF16 = jnp.bfloat16

SINE = [(-1.0) ** k * (math.pi / 2) ** (2 * k + 1) / math.factorial(2 * k + 1) for k in range(7)]


def basis(total, place, wave):
    turns = (2.0 * place + 1.0) * wave
    rest = turns - (4.0 * total) * jnp.floor(turns * (1.0 / (4.0 * total)))
    t = (jnp.abs(rest - 2.0 * total) - total) * (1.0 / total)
    t2 = t * t
    poly = jnp.full(t.shape, SINE[-1], F32)
    for c in SINE[-2::-1]:
        poly = poly * t2 + c
    scale = jnp.where(wave == 0.0, math.sqrt(1.0 / total), math.sqrt(2.0 / total))
    return scale * (poly * t)


def iota(shape, dim):
    return lax.broadcasted_iota(jnp.int32, shape, dim)


def split(x):
    hi = x.astype(BF16)
    return hi, (x - hi.astype(F32)).astype(BF16)


def group_masks(rows):
    lane = iota((rows, LANES), 1) // KY
    return [lane == g for g in range(LANES // KY)]


def plan(fields, n_in):
    slots = [range(f, min(f + n_in, fields)) for f in range(0, fields, n_in)]
    return slots, max(len(slots) - 2, 0)


def synthesize(coef, scale, weight_ref, row, col, numbers, variables, put):
    size, cols = coef.shape[0], col.shape[1]
    count = size // SUB
    groups = KX // SUB
    scaled = coef * scale
    stack = jnp.concatenate([jnp.where(m, scaled, 0.0) for m in group_masks(size)], axis=0)
    hi, lo = split(stack)
    lhs = jnp.concatenate([hi, lo, hi], axis=1)
    wave = jnp.dot(lhs, col, preferred_element_type=F32).reshape(groups, count, SUB, cols)
    for k, f in enumerate(numbers):
        whole = jnp.concatenate([wave[g, k] for g in range(groups)], axis=0)
        hi, lo = split(whole)
        rhs = jnp.concatenate([hi, lo, hi, lo], axis=0)
        recon = jnp.dot(row, rhs, preferred_element_type=F32)
        put(k, f, (weight_ref[f // variables] * recon).astype(BF16))


def analysis_kernel(
    dims, prog_hbm, forc_hbm, strength_hbm, level_hbm, pbl_hbm,
    coef_ref, scale_ref, weight_ref, row_ref, col_ref, early_ref,
    strength, level, pbl, prog, forc, part, mine, got_in, total, got_out, full,
    prog_sem, forc_sem, aux_sem, in_send, in_recv, out_send, out_recv, all_send, all_recv,
):
    gx, gy, n_mid, chunk = dims
    fields, rows, cols = prog.shape
    levels, variables = strength.shape
    n_chunks = fields // chunk
    groups = KX // SUB
    n_in, n_out = n_mid * gy, gx // n_mid
    slots, n_early = plan(fields, n_in)
    ix, iy = lax.axis_index("gx"), lax.axis_index("gy")
    outer, mid = ix // n_mid, lax.rem(ix, n_mid)
    me = mid * gy + iy

    def fetch(c):
        span = pl.ds(c * chunk, chunk)
        return (
            pltpu.make_async_copy(prog_hbm.at[span], prog.at[span], prog_sem.at[c]),
            pltpu.make_async_copy(forc_hbm.at[span], forc.at[span], forc_sem.at[c]),
        )

    for c in range(n_chunks):
        for copy in fetch(c):
            copy.start()
    aux = [
        pltpu.make_async_copy(pbl_hbm, pbl, aux_sem.at[0]),
        pltpu.make_async_copy(strength_hbm, strength, aux_sem.at[1]),
        pltpu.make_async_copy(level_hbm, level, aux_sem.at[2]),
    ]
    for copy in aux:
        copy.start()

    def inner_peer(d):
        other = lax.rem(me + d, n_in)
        return other, (outer * n_mid + other // gy, lax.rem(other, gy))

    def outer_peer(d):
        return (lax.rem(outer + d, n_out) * n_mid + mid, iy)

    def where_owned(s, owner, act):
        if len(slots[s]) == n_in:
            act()
        else:
            pl.when(owner < len(slots[s]))(act)

    barrier = pltpu.get_barrier_semaphore()
    for d in range(1, n_in):
        pl.semaphore_signal(barrier, inc=1, device_id=inner_peer(d)[1], device_id_type=MESH)
    for d in range(1, n_out):
        pl.semaphore_signal(barrier, inc=1, device_id=outer_peer(d), device_id_type=MESH)

    row = basis(
        rows * gx,
        (ix * rows + iota((KX, rows), 1)).astype(F32),
        iota((KX, rows), 0).astype(F32),
    )
    row_hi, row_lo = split(row)
    row_lhs = jnp.concatenate([row_hi, row_lo], axis=0)
    row_lhs = jnp.concatenate([row_lhs, row_lhs], axis=1)
    col = basis(
        cols * gy,
        (iy * cols + iota((cols, LANES), 0)).astype(F32),
        lax.rem(iota((cols, LANES), 1), KY).astype(F32),
    )
    col_rhs = jnp.concatenate(split(col), axis=1)

    def one_chunk(c, carry):
        for copy in fetch(c):
            copy.wait()
        for k in range(chunk):
            f = c * chunk + k
            diff = forc[f].astype(F32) - prog[f]
            rhs = jnp.concatenate(split(diff), axis=0)
            both = jnp.dot(row_lhs, rhs, preferred_element_type=F32)
            both = both[:KX] + both[KX:]
            for g in range(groups):
                part[g, f] = both[g * SUB:(g + 1) * SUB]
        return carry

    def to_owner(s, d):
        other, device = inner_peer(d)
        return other, pltpu.make_async_remote_copy(
            src_ref=mine.at[s, other], dst_ref=got_in.at[s, d - 1],
            send_sem=in_send.at[s, d - 1], recv_sem=in_recv.at[s, d - 1],
            device_id=device, device_id_type=MESH,
        )

    def to_plane(s, d):
        return pltpu.make_async_remote_copy(
            src_ref=total.at[s], dst_ref=got_out.at[s, d - 1],
            send_sem=out_send.at[s, d - 1], recv_sem=out_recv.at[s, d - 1],
            device_id=outer_peer(d), device_id_type=MESH,
        )

    def to_all(s, d):
        return pltpu.make_async_remote_copy(
            src_ref=full.at[s, me], dst_ref=full.at[s, me],
            send_sem=all_send.at[s, d - 1], recv_sem=all_recv.at[s, d - 1],
            device_id=inner_peer(d)[1], device_id_type=MESH,
        )

    for s, numbers in enumerate(slots):
        first, count = numbers[0], len(numbers)
        lax.fori_loop(first // chunk, (first + count) // chunk, one_chunk, 0)
        size = count * SUB
        hi, lo = split(part[:, first:first + count].reshape(groups * size, cols))
        both = jnp.dot(hi, col_rhs, preferred_element_type=F32) + jnp.dot(
            lo, col_rhs, preferred_element_type=F32
        )
        both = both[:, :LANES] + both[:, LANES:]
        coef = both[:size]
        for g, mask in list(enumerate(group_masks(size)))[1:]:
            coef = jnp.where(mask, both[g * size:(g + 1) * size], coef)
        for k in range(count):
            mine[s, k] = coef[k * SUB:(k + 1) * SUB]
        if s == 0:
            pl.semaphore_wait(barrier, n_in - 1 + n_out - 1)
        for d in range(1, n_in):
            other, copy = to_owner(s, d)
            where_owned(s, other, copy.start)

    for copy in aux:
        copy.wait()
    for l in range(levels):
        weight_ref[l] = 1.0 / (1.0 + jnp.exp(-(level[l] - pbl[...]) / RAMP_DEPTH))
        for v in range(variables):
            f = l * variables + v
            scale_ref[f * SUB:(f + 1) * SUB] = jnp.full((SUB, LANES), strength[l, v], F32)
    col_hi, col_lo = split(basis(
        cols * gy,
        (iy * cols + iota((LANES, cols), 1)).astype(F32),
        lax.rem(iota((LANES, cols), 0), KY).astype(F32),
    ))
    col_ref[...] = jnp.concatenate([col_hi, col_hi, col_lo], axis=0)
    row_hi, row_lo = split(basis(
        rows * gx,
        (ix * rows + iota((rows, 4 * KX), 0)).astype(F32),
        lax.rem(iota((rows, 4 * KX), 1), KX).astype(F32),
    ))
    row_ref[...] = jnp.where(
        iota((rows, 4 * KX), 1) < 2 * KX, row_hi.astype(F32), row_lo.astype(F32)
    ).astype(BF16)

    for s in range(len(slots)):
        def reduce_in(s=s):
            acc = mine[s, me]
            for d in range(1, n_in):
                to_owner(s, d)[1].wait_recv()
                acc = acc + got_in[s, d - 1]
            total[s] = acc
            for d in range(1, n_out):
                to_plane(s, d).start()
        where_owned(s, me, reduce_in)
    for s in range(len(slots)):
        def reduce_out(s=s):
            acc = total[s]
            for d in range(1, n_out):
                to_plane(s, d).wait_recv()
                acc = acc + got_out[s, d - 1]
            full[s, me] = acc
            for d in range(1, n_in):
                to_all(s, d).start()
        where_owned(s, me, reduce_out)
    for s, numbers in enumerate(slots):
        for d in range(1, n_in):
            sender = lax.rem(me + n_in - d, n_in)
            where_owned(s, sender, to_all(s, d).wait_recv)
        for k, f in enumerate(numbers):
            coef_ref[f * SUB:(f + 1) * SUB] = full[s, k]
        if s < n_early:
            span = slice(numbers[0] * SUB, (numbers[-1] + 1) * SUB)

            def keep(k, f, value):
                early_ref[f] = value

            synthesize(
                coef_ref[span], scale_ref[span], weight_ref, row_ref[...], col_ref[...],
                numbers, variables, keep,
            )
    for s in range(len(slots)):
        for d in range(1, n_in):
            other, copy = to_owner(s, d)
            where_owned(s, other, copy.wait_send)

        def sent(s=s):
            for d in range(1, n_out):
                to_plane(s, d).wait_send()
            for d in range(1, n_in):
                to_all(s, d).wait_send()
        where_owned(s, me, sent)


def synthesis_kernel(
    done, coef_ref, scale_ref, weight_ref, row_ref, col_ref, early_ref, tend_hbm, energy_ref,
    tend, tend_sem,
):
    levels, variables = energy_ref.shape
    fields = levels * variables

    def out(f):
        source = early_ref.at[f] if f < done else tend.at[f - done]
        return pltpu.make_async_copy(
            source, tend_hbm.at[f // variables, f % variables], tend_sem.at[f]
        )

    for f in range(done):
        out(f).start()

    def keep(k, f, value):
        tend[f - done] = value
        if k:
            out(f - 1).start()

    coef = coef_ref[...]
    synthesize(
        coef[done * SUB:], scale_ref[done * SUB:], weight_ref, row_ref[...], col_ref[...],
        range(done, fields), variables, keep,
    )
    out(fields - 1).start()

    power = coef * coef
    at_row = iota((levels, variables), 0)
    at_col = iota((levels, variables), 1)
    energy = jnp.zeros((levels, variables), F32)
    for l in range(levels):
        for v in range(variables):
            f = l * variables + v
            one = jnp.sum(power[f * SUB:(f + 1) * SUB], axis=(0, 1), keepdims=True)
            energy = jnp.where((at_row == l) & (at_col == v), one, energy)
    energy_ref[...] = energy * (1.0 / (KX * KY))

    for f in range(fields):
        out(f).wait()


def per_device(gx, gy, prognostic_values, forcing_host_values, strength, level_height, pbl_height):
    levels, variables, rows, cols = prognostic_values.shape
    fields = levels * variables
    groups = KX // SUB
    n_mid = gx
    n_in, n_out = n_mid * gy, gx // n_mid
    slots, n_early = plan(fields, n_in)
    n_slots = len(slots)
    done = n_early * n_in
    chunk = math.gcd(fields, n_in)
    n_chunks = fields // chunk
    near, far = max(n_in - 1, 1), max(n_out - 1, 1)
    anywhere = pl.BlockSpec(memory_space=pl.ANY)
    vmem = pl.BlockSpec(memory_space=pltpu.VMEM)
    dma = pltpu.SemaphoreType.DMA
    held = pl.pallas_call(
        functools.partial(analysis_kernel, (gx, gy, n_mid, chunk)),
        out_shape=(
            pltpu.VMEM((fields * SUB, LANES), F32),
            pltpu.VMEM((fields * SUB, LANES), F32),
            pltpu.VMEM((levels, rows, cols), F32),
            pltpu.VMEM((rows, 4 * KX), BF16),
            pltpu.VMEM((3 * LANES, cols), BF16),
            pltpu.VMEM((max(done, 1), rows, cols), BF16),
        ),
        in_specs=[anywhere] * 5,
        out_specs=(vmem,) * 6,
        scratch_shapes=[
            pltpu.SMEM((levels, variables), F32),
            pltpu.SMEM((levels,), F32),
            pltpu.VMEM((rows, cols), F32),
            pltpu.VMEM((fields, rows, cols), F32),
            pltpu.VMEM((fields, rows, cols), BF16),
            pltpu.VMEM((groups, fields, SUB, cols), F32),
            pltpu.VMEM((n_slots, n_in, SUB, LANES), F32),
            pltpu.VMEM((n_slots, near, SUB, LANES), F32),
            pltpu.VMEM((n_slots, SUB, LANES), F32),
            pltpu.VMEM((n_slots, far, SUB, LANES), F32),
            pltpu.VMEM((n_slots, n_in, SUB, LANES), F32),
            dma((n_chunks,)),
            dma((n_chunks,)),
            dma((3,)),
            dma((n_slots, near)),
            dma((n_slots, near)),
            dma((n_slots, far)),
            dma((n_slots, far)),
            dma((n_slots, near)),
            dma((n_slots, near)),
        ],
        compiler_params=pltpu.CompilerParams(collective_id=0, has_side_effects=True),
        name="analysis",
    )(
        prognostic_values.reshape(fields, rows, cols),
        forcing_host_values.reshape(fields, rows, cols),
        strength,
        level_height,
        pbl_height,
    )
    tendency, energy = pl.pallas_call(
        functools.partial(synthesis_kernel, done),
        out_shape=(
            jax.ShapeDtypeStruct((levels, variables, rows, cols), BF16),
            jax.ShapeDtypeStruct((levels, variables), F32),
        ),
        in_specs=[vmem] * 6,
        out_specs=(anywhere, vmem),
        scratch_shapes=[
            pltpu.VMEM((fields - done, rows, cols), BF16),
            dma((fields,)),
        ],
        name="synthesis",
    )(*[pltpu.with_memory_space_constraint(x, pltpu.VMEM) for x in held])
    return tendency, energy


def solution(mesh):
    return jax.shard_map(
        functools.partial(per_device, mesh.shape["gx"], mesh.shape["gy"]),
        mesh=mesh,
        in_specs=(P(None, None, "gx", "gy"), P(None, None, "gx", "gy"), P(), P(), P("gx", "gy")),
        out_specs=(P(None, None, "gx", "gy"), P()),
        check_vma=False,
    )
```

time: 22 us -> 20.8 us (0.945)
  Pallas kernels: 21.2 us -> 20 us
    pallas_call x1, Pallas kernels: 18.1 us -> 17.2 us  [per_device(): pl.pallas_call(functools.partial(analysis_kernel, (gx, gy, n_mid, chunk))...]
    pallas_call x1, Pallas kernels: 3.03 us -> 2.78 us  [per_device(): pl.pallas_call(functools.partial(synthesis_kernel, done), out_shape=(jax....]
where the time goes in v3:
time: 20.8 us; the launch traced here: 20.6 us
  Pallas kernels  20 us (96%)
  between operations  0.64 us (3%)
    pallas_call x1, Pallas kernels, per_device(): pl.pallas_call(functools.partial(analysis_kernel, (gx, gy, n_mid, chunk))...  17.2 us
    pallas_call x1, Pallas kernels, per_device(): pl.pallas_call(functools.partial(synthesis_kernel, done), out_shape=(jax....  2.78 us

profile of v3, /device:TPU:0, one launch (start us, length us, event | category | flops | bytes accessed | tf_op | source)
XLA Modules:
  0.0 20.6 jit_solution(4360658843444845566)
XLA Ops:
  0.6 17.2 %analysis.1 = (f32[144,128]{1,0:T(8,128)S(1)}, f32[144,128]{1,0:T(8,128)S(1)}, f32[3,128,512]{2,1,0:T(8,128)S(1)}, bf16[128,128]{1,0:T(8,128)(2,1)S(1)}, bf16[38...) custom-call(f32[18,128,512]{2,1,0:T(8,128)} %bitcast.2, bf16[18,128,512]{2,1,0:T(8,128)(2,1)} %bitcast.3, ...), custom_call_target="tpu_custom_call" | custom-call | tf_op jit(solution)/shard_map/analysis/pallas_call | solution.py:325
  17.9 2.8 %synthesis.1 = (bf16[3,6,128,512]{3,2,1,0:T(8,128)(2,1)}, f32[3,6]{1,0:T(4,128)}) custom-call(f32[144,128]{1,0:T(8,128)S(1)} %get-tuple-element.8.coef_ref, f32[144,128]{1,0:T(8,128)S(1)} %get-tuple-element.9.scale_ref, f32[3,128,512]{2,1,0:T(8,128)S(1)} %get-tuple-element.10.weight_ref, bf16[128,128]{1,0:T(8,128)(2,1)S(1)} %get-tuple-element.11.row_ref, ...), custom_call_target="tpu_custom_call" | custom-call | tf_op jit(solution)/shard_map/synthesis/pallas_call | solution.py:368
